TPU v7x, 16 devices: a 4x2x1 block of a 4x4x8 slice. The times are simulated.
16 devices in a mesh: dp: 2 (over y, z), sp: 8 (over x, core).
Axes of the slice: x: 4, y: 2, z: 1, core: 2. Of those that a mesh axis runs over, the one named last changes fastest.
The devices are a block of a 4x4x8 slice.
Arguments:
- x: bfloat16 [4096, 2048], P(('dp', 'sp')), parts along dimension 0
- doc_start: int32 [4096], P(('dp', 'sp')), parts along dimension 0
- w_in: bfloat16 [2048, 8384], replicated
- conv_w: float32 [4, 4224], replicated
- conv_b: float32 [4224], replicated
- dt_bias: float32 [64], replicated
- a_log: float32 [64], replicated
- d_skip: float32 [64], replicated
- norm_w: float32 [1, 4096], replicated
- w_out: bfloat16 [4096, 2048], replicated
Outputs:
- output: bfloat16 [4096, 2048], P(('dp', 'sp')), parts along dimension 0
There are 2 independent parts. A program takes and returns all parts, laid end to end along the dimension named above; an argument that names none is the same for every part.
All inputs are finite; a program needn't handle non-finite values.
Results may differ from a plain program's by a relative error of at most 0.00405549.
Values are sent between devices in bfloat16 or wider.
A program may use at most 768 MiB of HBM per device.

v0:
```python
import math
import jax
import jax.numpy as jnp
from jax import lax
from jax.sharding import PartitionSpec as P

CHUNK_LEN = 256
NORM_EPS = 1e-5


def conv_halo_rows(conv_in, keep_flag, conv_width):
    n_tok = conv_in.shape[0]
    tail_keep = jnp.cumprod(keep_flag[n_tok - conv_width + 2:][::-1])[::-1]
    tail_ok = jnp.concatenate([tail_keep, jnp.ones((1,), jnp.float32)])
    last_rows = conv_in[n_tok - conv_width + 1:]
    return jnp.where(tail_ok[:, None] > 0.5, last_rows, jnp.zeros_like(last_rows))


def causal_conv(conv_in, halo_rows, keep_flag, conv_w, conv_b):
    conv_width = conv_w.shape[0]
    n_tok = conv_in.shape[0]
    ext_rows = jnp.concatenate([halo_rows, conv_in], axis=0)
    keep_ext = jnp.concatenate([jnp.ones((conv_width - 1,), jnp.float32), keep_flag])
    pre_act = conv_b + conv_w[0] * conv_in
    tap_mask = jnp.ones((n_tok,), jnp.float32)
    for offset in range(1, conv_width):
        tap_mask = tap_mask * keep_ext[conv_width - offset:conv_width - offset + n_tok]
        pre_act = pre_act + conv_w[offset] * (tap_mask[:, None] * ext_rows[conv_width - 1 - offset:conv_width - 1 - offset + n_tok])
    return jax.nn.silu(pre_act).astype(jnp.bfloat16)


def local_scan(conv_out, dt_val, doc_start, a_log, groups, d_inner):
    n_tok = conv_out.shape[0]
    n_heads = a_log.shape[0]
    per_group = n_heads // groups
    head_dim = d_inner // n_heads
    state_dim = (conv_out.shape[1] - d_inner) // (2 * groups)
    n_chunks = n_tok // CHUNK_LEN
    xs_chunk = conv_out[:, :d_inner].reshape(n_chunks, CHUNK_LEN, groups, per_group, head_dim)
    b_chunk = conv_out[:, d_inner:d_inner + groups * state_dim].reshape(n_chunks, CHUNK_LEN, groups, state_dim)
    c_chunk = conv_out[:, d_inner + groups * state_dim:].reshape(n_chunks, CHUNK_LEN, groups, state_dim)
    dt_chunk = dt_val.reshape(n_chunks, CHUNK_LEN, groups, per_group)
    cum_decay = jnp.cumsum(-jnp.exp(a_log).reshape(groups, per_group) * dt_chunk, axis=1)
    seg_ids = jnp.cumsum(doc_start.reshape(n_chunks, CHUNK_LEN), axis=1)
    position = jnp.arange(CHUNK_LEN)
    allowed = (position[:, None] >= position[None, :]) & (seg_ids[:, :, None] == seg_ids[:, None, :])
    cum_rows = jnp.moveaxis(cum_decay, 1, -1)
    decay_mat = jnp.exp(jnp.where(allowed[:, None, None], cum_rows[..., :, None] - cum_rows[..., None, :], -jnp.inf))
    scores = jnp.einsum('cign,cjgn->cgij', c_chunk, b_chunk, preferred_element_type=jnp.float32)
    mix_mat = (scores[:, :, None] * decay_mat * jnp.moveaxis(dt_chunk, 1, -1)[..., None, :]).astype(jnp.bfloat16)
    y_intra = jnp.einsum('cgkij,cjgkp->cigkp', mix_mat, xs_chunk, preferred_element_type=jnp.float32)
    last_cum = cum_decay[:, -1]
    end_same = seg_ids == seg_ids[:, -1:]
    w_end = jnp.exp(last_cum[:, None] - cum_decay) * dt_chunk * end_same[..., None, None]
    scaled_x = (xs_chunk * w_end[..., None]).astype(jnp.bfloat16)
    chunk_state = jnp.einsum('cjgkp,cjgn->cgkpn', scaled_x, b_chunk, preferred_element_type=jnp.float32)
    chunk_reset = (seg_ids[:, -1] > 0).astype(jnp.int32)
    chunk_decay = jnp.exp(last_cum) * (chunk_reset == 0)[:, None, None]
    cum_in = jnp.cumsum(last_cum, axis=0)
    cum_ex = cum_in - last_cum
    reset_in = jnp.cumsum(chunk_reset)
    reset_ex = reset_in - chunk_reset
    chunk_idx = jnp.arange(n_chunks)
    link_ok = (chunk_idx[:, None] > chunk_idx[None, :]) & (reset_ex[:, None] == reset_in[None, :])
    carry_w = jnp.exp(jnp.where(link_ok[:, :, None, None], cum_ex[:, None] - cum_in[None, :], -jnp.inf))
    local_start = jnp.einsum('cdgk,dgkpn->cgkpn', carry_w, chunk_state, precision=lax.Precision.HIGHEST)
    start_decay = jnp.exp(cum_ex) * (reset_ex == 0)[:, None, None]
    w_start = jnp.exp(cum_decay) * (seg_ids == 0)[..., None, None]
    return y_intra, local_start, start_decay, w_start, c_chunk, chunk_state, chunk_decay


def finish_layer(y_intra, local_start, start_decay, w_start, c_chunk, state_in, conv_out, gate_in, d_skip, norm_w, w_out):
    n_tok = conv_out.shape[0]
    n_heads = d_skip.shape[0]
    groups, group_width = norm_w.shape
    d_inner = groups * group_width
    head_dim = d_inner // n_heads
    start_states = local_start + start_decay[..., None, None] * state_in
    y_state = jnp.einsum('cign,cgkpn->cigkp', c_chunk, start_states.astype(jnp.bfloat16), preferred_element_type=jnp.float32) * w_start[..., None]
    y_heads = (y_intra + y_state).reshape(n_tok, n_heads, head_dim) + d_skip[:, None] * conv_out[:, :d_inner].reshape(n_tok, n_heads, head_dim)
    gated_y = y_heads.reshape(n_tok, groups, group_width) * jax.nn.silu(gate_in.astype(jnp.float32)).reshape(n_tok, groups, group_width)
    normed = gated_y * lax.rsqrt(jnp.mean(gated_y * gated_y, axis=-1, keepdims=True) + NORM_EPS) * norm_w
    return jnp.dot(normed.reshape(n_tok, d_inner).astype(jnp.bfloat16), w_out, preferred_element_type=jnp.float32).astype(jnp.bfloat16)


def solution(mesh):
    n_seq = mesh.shape['sp']
    n_rounds = int(math.ceil(math.log2(n_seq)))
    next_pairs = [(source, source + 1) for source in range(n_seq - 1)]
    row_spec = P(('dp', 'sp'), None)
    tok_spec = P(('dp', 'sp'))

    def layer_shard(x, doc_start, w_in, conv_w, conv_b, dt_bias, a_log, d_skip, norm_w, w_out):
        groups = norm_w.shape[0]
        d_inner = norm_w.shape[0] * norm_w.shape[1]
        conv_dim = conv_w.shape[1]
        seq_rank = lax.axis_index('sp')
        projected = jnp.dot(x, w_in, preferred_element_type=jnp.float32).astype(jnp.bfloat16)
        conv_in = projected[:, d_inner:d_inner + conv_dim]
        keep_flag = (1 - doc_start).astype(jnp.float32)
        halo_rows = lax.ppermute(conv_halo_rows(conv_in, keep_flag, conv_w.shape[0]), 'sp', next_pairs)
        conv_out = causal_conv(conv_in, halo_rows, keep_flag, conv_w, conv_b)
        dt_val = jax.nn.softplus(projected[:, d_inner + conv_dim:].astype(jnp.float32) + dt_bias)
        pieces = local_scan(conv_out, dt_val, doc_start, a_log, groups, d_inner)
        y_intra, local_start, start_decay, w_start, c_chunk, chunk_state, chunk_decay = pieces
        acc_decay = start_decay[-1] * chunk_decay[-1]
        acc_state = chunk_decay[-1][..., None, None] * local_start[-1] + chunk_state[-1]
        for round_idx in range(n_rounds):
            hop_len = 2 ** round_idx
            hop_pairs = [(source, source + hop_len) for source in range(n_seq - hop_len)]
            got_decay = lax.ppermute(acc_decay, 'sp', hop_pairs)
            got_state = lax.ppermute(acc_state, 'sp', hop_pairs)
            got_decay = jnp.where(seq_rank >= hop_len, got_decay, 1.0)
            acc_state = acc_decay[..., None, None] * got_state + acc_state
            acc_decay = got_decay * acc_decay
        state_in = lax.ppermute(acc_state, 'sp', next_pairs)
        return finish_layer(y_intra, local_start, start_decay, w_start, c_chunk, state_in, conv_out, projected[:, :d_inner], d_skip, norm_w, w_out)

    return jax.shard_map(layer_shard, mesh=mesh, in_specs=(row_spec, tok_spec, P(), P(), P(), P(), P(), P(), P(), P()), out_specs=row_spec, check_vma=False)
```

profile of v0, /device:TPU:113, one launch (start us, length us, event | category | flops | bytes accessed | tf_op | source)
XLA Modules:
  0.0 245.2 jit_solution(3779757667110506247)
XLA Ops:
  1.3 17.0 %convolution_convert_fusion = bf16[256,8384]{1,0:T(8,128)(2,1)} fusion(bf16[256,2048]{1,0:T(8,128)(2,1)S(1)} %copy-done, bf16[2048,8384]{0,1:T(8,128)(2,1)} %param.12), kind=kOutput, calls=%fused_computation.1 | convolution fusion | flops 8793407488 | bytes 39682048 | tf_op jit(solution)/shard_map/dot_general | solution.py:98
  19.3 4.6 %collective-permute-start = (bf16[3,4224]{1,0:T(4,128)(2,1)S(1)}, bf16[3,4224]{1,0:T(4,128)(2,1)S(1)}, u32[]{:S(2)}, u32[]{:S(2)}) collective-permute-start(bf16[3,4224]{1,0:T(4,128)(2,1)S(1)} %slice_select_fusion), channel_id=1, source_target_pairs={{0,1},{1,2},{2,3},{3,4},{4,5},{5,6},{6,7},{8,9},{9,10},{10,11},{11... | collective-permute-start | bytes 76040 | tf_op jit(solution)/shard_map/ppermute | solution.py:101
  30.5 3.1 %slice.95 = bf16[256,4224]{1,0:T(8,128)(2,1)} slice(bf16[256,8384]{1,0:T(8,128)(2,1)} %convolution_convert_fusion), slice={[0:256], [4096:8320]} | slice | bytes 4325376 | tf_op jit(solution)/shard_map/slice | solution.py:99
  33.7 2.3 mul.364
  36.0 5.7 %copy.46 = f32[256,4096]{1,0:T(8,128)} copy(f32[256,4096]{0,1:T(8,128)} %bitcast.103) | data formatting | bytes 8388608 | tf_op jit(solution)/shard_map/mul | solution.py:55
  41.7 8.5 %multiply_convert_fusion.2 = bf16[256,4224]{1,0:T(8,128)(2,1)S(1)} fusion(bf16[256,4224]{1,0:T(8,128)(2,1)} %slice.95, bf16[3,4224]{1,0:T(4,128)(2,1)S(1)} %collective-permute-done, f32[256]{0:T(256)S(1)} %get-tuple-element.15, f32[4224]{0:T(1024)S(1)} %get-tuple-element.7, f32[256]{0:T(256)S(1)} %get-tuple-element.16, f32[4224]{0:T(1024)S(1)} %get-tuple-element.8, ...), kind=kLoop, calls=%fused_computation.13 | loop fusion | flops 31358976 | bytes 4438272 | tf_op jit(solution)/shard_map/convert_element_type | solution.py:29
  52.2 4.1 %copy.47 = bf16[256,4096]{0,1:T(8,128)(2,1)} copy(bf16[256,4096]{1,0:T(8,128)(2,1)} %fusion.7) | data formatting | bytes 4194304 | tf_op jit(solution)/shard_map/convert_element_type | solution.py:55
  56.3 2.3 fusion.28
  60.8 22.9 %collective-permute-done.3 = f32[1,64,64,64]{3,2,1,0:T(8,128)S(1)} collective-permute-done((f32[1,64,64,64]{3,2,1,0:T(8,128)S(1)}, f32[1,64,64,64]{3,2,1,0:T(8,128)S(1)}, u32[]{:S(2)}, u32[]{:S(2)}) %collective-permute-start.3) | collective-permute-done | bytes 1048608 | tf_op jit(solution)/shard_map/ppermute | solution.py:112
  85.4 4.8 %collective-permute-start.4 = (f32[1,64,64,64]{3,2,1,0:T(8,128)}, f32[1,64,64,64]{3,2,1,0:T(8,128)}, u32[]{:S(2)}, u32[]{:S(2)}) collective-permute-start(f32[1,64,64,64]{3,2,1,0:T(8,128)} %multiply_add_fusion.3), channel_id=1, source_target_pairs={{0,2},{1,3},{2,4},{3,5},{4,6},{5,7},{8,10},{9,11},{10,12},{11,13},... | collective-permute-start | bytes 3145736 | tf_op jit(solution)/shard_map/ppermute | solution.py:112
  90.2 3.4 %collective-permute-start.1 = (f32[1,64]{1,0:T(1,128)S(1)}, f32[1,64]{1,0:T(1,128)S(1)}, u32[]{:S(2)}, u32[]{:S(2)}) collective-permute-start(f32[1,64]{1,0:T(1,128)S(1)} %get-tuple-element.22), channel_id=1, source_target_pairs={{0,1},{1,2},{2,3},{3,4},{4,5},{5,6},{6,7},{8,9},{9,10},{10,11},{11... | collective-permute-start | bytes 776 | tf_op jit(solution)/shard_map/ppermute | solution.py:111
  93.6 39.0 %collective-permute-done.1 = f32[1,64]{1,0:T(1,128)S(1)} collective-permute-done((f32[1,64]{1,0:T(1,128)S(1)}, f32[1,64]{1,0:T(1,128)S(1)}, u32[]{:S(2)}, u32[]{:S(2)}) %collective-permute-start.1) | collective-permute-done | bytes 288 | tf_op jit(solution)/shard_map/ppermute | solution.py:111
  132.6 3.8 %multiply_add_fusion.2 = f32[1,64,64,64]{3,2,1,0:T(8,128)} fusion(f32[1,64,64,64]{3,2,1,0:T(8,128)} %multiply_add_fusion.3, f32[1,64,64,64]{3,2,1,0:T(8,128)} %collective-permute-done.4, f32[64]{0:T(128)S(1)} %bitcast.112), kind=kLoop, calls=%fused_computation.38 | loop fusion | flops 524288 | bytes 3145984 | tf_op jit(solution)/shard_map/add | solution.py:114
  136.4 6.7 %collective-permute-start.5 = (f32[1,64,64,64]{3,2,1,0:T(8,128)}, f32[1,64,64,64]{3,2,1,0:T(8,128)}, u32[]{:S(2)}, u32[]{:S(2)}) collective-permute-start(f32[1,64,64,64]{3,2,1,0:T(8,128)} %multiply_add_fusion.2), channel_id=1, source_target_pairs={{0,4},{1,5},{2,6},{3,7},{8,12},{9,13},{10,14},{11,15}} | collective-permute-start | bytes 3145736 | tf_op jit(solution)/shard_map/ppermute | solution.py:112
  145.0 39.4 %collective-permute-done.2 = f32[1,64]{1,0:T(1,128)S(1)} collective-permute-done((f32[1,64]{1,0:T(1,128)S(1)}, f32[1,64]{1,0:T(1,128)S(1)}, u32[]{:S(2)}, u32[]{:S(2)}) %collective-permute-start.2) | collective-permute-done | bytes 288 | tf_op jit(solution)/shard_map/ppermute | solution.py:111
  186.0 4.1 %copy.39 = bf16[256,4096]{0,1:T(8,128)(2,1)} copy(bf16[256,4096]{1,0:T(8,128)(2,1)} %slice.101) | data formatting | bytes 4194304 | tf_op jit(solution)/shard_map/slice | solution.py:39
  190.0 2.6 %multiply_add_fusion.1 = f32[1,64,64,64]{3,2,1,0:T(8,128)S(1)} fusion(f32[1,64,64,64]{3,2,1,0:T(8,128)} %multiply_add_fusion.2, f32[1,64,64,64]{3,2,1,0:T(8,128)} %collective-permute-done.5, f32[64]{0:T(128)S(1)} %fusion.39), kind=kLoop, calls=%fused_computation.37 | loop fusion | flops 524288 | bytes 3145984 | tf_op jit(solution)/shard_map/add | solution.py:114
  192.7 7.6 %collective-permute-start.6 = (f32[1,64,64,64]{3,2,1,0:T(8,128)S(1)}, f32[1,64,64,64]{3,2,1,0:T(8,128)S(1)}, u32[]{:S(2)}, u32[]{:S(2)}) collective-permute-start(f32[1,64,64,64]{3,2,1,0:T(8,128)S(1)} %multiply_add_fusion.1), channel_id=1, source_target_pairs={{0,1},{1,2},{2,3},{3,4},{4,5},{5,6},{6,7},{8,9},{9,10},{10,11},{11... | collective-permute-start | bytes 3145736 | tf_op jit(solution)/shard_map/ppermute | solution.py:116
  200.5 4.4 %fusion = f32[64,64,256]{2,1,0:T(8,128)S(1)} fusion(bf16[256,64,64]{0,2,1:T(8,128)(2,1)S(1)} %bitcast.105, f32[64,256]{1,0:T(8,128)S(1)} %copy.43, f32[64,256]{1,0:T(8,128)S(1)} %bitcast_add_fusion.1, f32[256,256]{1,0:T(8,128)S(1)} %fusion.31, pred[256,256]{1,0:T(8,128)(4,1)S(1)} %fusion.24), kind=kOutput, calls=%fused_computation.2 | convolution fusion | flops 557842432 | bytes 6750208 | tf_op jit(solution)/shard_map/cgkij,cjgkp->cigkp/dot_general | solution.py:51
  205.0 18.0 %collective-permute-done.6 = f32[1,64,64,64]{3,2,1,0:T(8,128)S(1)} collective-permute-done((f32[1,64,64,64]{3,2,1,0:T(8,128)S(1)}, f32[1,64,64,64]{3,2,1,0:T(8,128)S(1)}, u32[]{:S(2)}, u32[]{:S(2)}) %collective-permute-start.6) | collective-permute-done | bytes 1048608 | tf_op jit(solution)/shard_map/ppermute | solution.py:116
  223.0 2.8 %fusion.13 = f32[1,256,1,64,64]{1,4,3,2,0:T(8,128)} fusion(f32[64,64,256]{2,1,0:T(8,128)S(1)} %fusion, f32[256,64]{0,1:T(8,128)S(1)} %copy.50, f32[1,64,64,64]{3,2,1,0:T(8,128)S(1)} %collective-permute-done.6, f32[64,64,64]{2,1,0:T(8,128)S(1)} %copy-done.3, f32[64]{0:T(128)S(1)} %get-tuple-element.19, bf16[256,4224]{1,0:T(8,128)(2,1)S(1)} %multiply_convert_fusion.2), kind=kOutput, calls=%fused_computation.21 | convolution fusion | flops 137363456 | bytes 12714496 | tf_op jit(solution)/shard_map/cign,cgkpn->cigkp/dot_general | solution.py:79
  225.8 5.7 %copy.51 = f32[256,4096]{1,0:T(8,128)} copy(f32[256,4096]{0,1:T(8,128)} %bitcast.102) | data formatting | bytes 8388608 | tf_op jit(solution)/shard_map/reshape | solution.py:80
  231.5 4.2 %multiply_reduce_fusion = (f32[256]{0:T(256)S(1)}, f32[256,4096]{1,0:T(8,128)S(1)}) fusion(bf16[256,8384]{1,0:T(8,128)(2,1)} %convolution_convert_fusion, f32[256,4096]{1,0:T(8,128)} %copy.51, bf16[256,4224]{1,0:T(8,128)(2,1)S(1)} %multiply_convert_fusion.2, f32[4096]{0:T(1024)S(1)} %mul.399), kind=kLoop, calls=%fused_computation.23 | loop fusion | flops 11534080 | bytes 12600320 | tf_op jit(solution)/shard_map/reduce_sum | solution.py:82
  235.8 9.4 %convolution_convert_fusion.1 = bf16[256,2048]{1,0:T(8,128)(2,1)} fusion(bf16[4096,2048]{1,0:T(8,128)(2,1)} %param.19, f32[256,4096]{1,0:T(8,128)S(1)} %get-tuple-element.10, f32[4096]{0:T(1024)S(1)} %bitcast.116, f32[256]{0:T(256)S(1)} %add_rsqrt_fusion), kind=kOutput, calls=%fused_computation.27 | convolution fusion | flops 4298637312 | bytes 22037504 | tf_op jit(solution)/shard_map/dot_general | solution.py:83
  (79 shorter events, 17.2 us)
Async XLA Ops:
  0.0 1.2 copy-start
  1.2 22.6 %copy-start.12 = (f32[64]{0:T(128)S(1)}, f32[64]{0:T(128)}, u32[]{:S(2)}) copy-start(f32[64]{0:T(128)} %param.16) | copy-start | bytes 772
  1.2 22.6 %copy-start.9 = (f32[64]{0:T(128)S(1)}, f32[64]{0:T(128)}, u32[]{:S(2)}) copy-start(f32[64]{0:T(128)} %param.15) | copy-start | bytes 772
  1.2 24.6 %copy-start.8 = (s32[256]{0:T(256)S(1)}, s32[256]{0:T(256)}, u32[]{:S(2)}) copy-start(s32[256]{0:T(256)} %param.11) | copy-start | bytes 3076
  1.2 29.1 %copy-start.6 = (f32[4,4224]{1,0:T(4,128)S(1)}, f32[4,4224]{1,0:T(4,128)}, u32[]{:S(2)}) copy-start(f32[4,4224]{1,0:T(4,128)} %param.13) | copy-start | bytes 202756
  19.3 22.4 %collective-permute-start = (bf16[3,4224]{1,0:T(4,128)(2,1)S(1)}, bf16[3,4224]{1,0:T(4,128)(2,1)S(1)}, u32[]{:S(2)}, u32[]{:S(2)}) collective-permute-start(bf16[3,4224]{1,0:T(4,128)(2,1)S(1)} %slice_select_fusion), channel_id=1, source_target_pairs={{0,1},{1,2},{2,3},{3,4},{4,5},{5,6},{6,7},{8,9},{9,10},{10,11},{11... | collective-permute-start | bytes 76040 | tf_op jit(solution)/shard_map/ppermute | solution.py:101
  36.0 5.7 %copy-start.7 = (f32[4224]{0:T(1024)S(1)}, f32[4224]{0:T(1024)}, u32[]{:S(2)}) copy-start(f32[4224]{0:T(1024)} %param.14) | copy-start | bytes 50692
  41.7 8.5 %copy-start.4 = (f32[256,4096]{1,0:T(8,128)S(1)}, f32[256,4096]{1,0:T(8,128)}, u32[]{:S(2)}) copy-start(f32[256,4096]{1,0:T(8,128)} %copy.46) | copy-start | bytes 12582916
  58.6 26.9 %copy-start.2 = (f32[64,64,64]{2,1,0:T(8,128)}, f32[64,64,64]{2,1,0:T(8,128)S(1)}, u32[]{:S(2)}) copy-start(f32[64,64,64]{2,1,0:T(8,128)S(1)} %fusion.28) | copy-start | bytes 3145732
  58.8 24.9 %collective-permute-start.3 = (f32[1,64,64,64]{3,2,1,0:T(8,128)S(1)}, f32[1,64,64,64]{3,2,1,0:T(8,128)S(1)}, u32[]{:S(2)}, u32[]{:S(2)}) collective-permute-start(f32[1,64,64,64]{3,2,1,0:T(8,128)S(1)} %fusion.16), channel_id=1, source_target_pairs={{0,1},{1,2},{2,3},{3,4},{4,5},{5,6},{6,7},{8,9},{9,10},{10,11},{11... | collective-permute-start | bytes 3145736 | tf_op jit(solution)/shard_map/ppermute | solution.py:112
  85.4 59.4 %copy-start.10 = (f32[64]{0:T(128)S(1)}, f32[64]{0:T(128)}, u32[]{:S(2)}) copy-start(f32[64]{0:T(128)} %param.17) | copy-start | bytes 772
  85.4 47.1 %collective-permute-start.4 = (f32[1,64,64,64]{3,2,1,0:T(8,128)}, f32[1,64,64,64]{3,2,1,0:T(8,128)}, u32[]{:S(2)}, u32[]{:S(2)}) collective-permute-start(f32[1,64,64,64]{3,2,1,0:T(8,128)} %multiply_add_fusion.3), channel_id=1, source_target_pairs={{0,2},{1,3},{2,4},{3,5},{4,6},{5,7},{8,10},{9,11},{10,12},{11,13},... | collective-permute-start | bytes 3145736 | tf_op jit(solution)/shard_map/ppermute | solution.py:112
  90.2 42.3 %collective-permute-start.1 = (f32[1,64]{1,0:T(1,128)S(1)}, f32[1,64]{1,0:T(1,128)S(1)}, u32[]{:S(2)}, u32[]{:S(2)}) collective-permute-start(f32[1,64]{1,0:T(1,128)S(1)} %get-tuple-element.22), channel_id=1, source_target_pairs={{0,1},{1,2},{2,3},{3,4},{4,5},{5,6},{6,7},{8,9},{9,10},{10,11},{11... | collective-permute-start | bytes 776 | tf_op jit(solution)/shard_map/ppermute | solution.py:111
  136.4 53.6 %collective-permute-start.5 = (f32[1,64,64,64]{3,2,1,0:T(8,128)}, f32[1,64,64,64]{3,2,1,0:T(8,128)}, u32[]{:S(2)}, u32[]{:S(2)}) collective-permute-start(f32[1,64,64,64]{3,2,1,0:T(8,128)} %multiply_add_fusion.2), channel_id=1, source_target_pairs={{0,4},{1,5},{2,6},{3,7},{8,12},{9,13},{10,14},{11,15}} | collective-permute-start | bytes 3145736 | tf_op jit(solution)/shard_map/ppermute | solution.py:112
  143.4 41.0 %collective-permute-start.2 = (f32[1,64]{1,0:T(1,128)S(1)}, f32[1,64]{1,0:T(1,128)S(1)}, u32[]{:S(2)}, u32[]{:S(2)}) collective-permute-start(f32[1,64]{1,0:T(1,128)S(1)} %fusion.40), channel_id=1, source_target_pairs={{0,2},{1,3},{2,4},{3,5},{4,6},{5,7},{8,10},{9,11},{10,12},{11,13},... | collective-permute-start | bytes 776 | tf_op jit(solution)/shard_map/ppermute | solution.py:111
  190.0 10.5 %copy-start.5 = (bf16[256,4096]{0,1:T(8,128)(2,1)S(1)}, bf16[256,4096]{0,1:T(8,128)(2,1)}, u32[]{:S(2)}) copy-start(bf16[256,4096]{0,1:T(8,128)(2,1)} %copy.39) | copy-start | bytes 6291460
  192.7 30.4 %collective-permute-start.6 = (f32[1,64,64,64]{3,2,1,0:T(8,128)S(1)}, f32[1,64,64,64]{3,2,1,0:T(8,128)S(1)}, u32[]{:S(2)}, u32[]{:S(2)}) collective-permute-start(f32[1,64,64,64]{3,2,1,0:T(8,128)S(1)} %multiply_add_fusion.1), channel_id=1, source_target_pairs={{0,1},{1,2},{2,3},{3,4},{4,5},{5,6},{6,7},{8,9},{9,10},{10,11},{11... | collective-permute-start | bytes 3145736 | tf_op jit(solution)/shard_map/ppermute | solution.py:116
  200.5 22.5 %copy-start.3 = (f32[64,64,64]{2,1,0:T(8,128)S(1)}, f32[64,64,64]{2,1,0:T(8,128)}, u32[]{:S(2)}) copy-start(f32[64,64,64]{2,1,0:T(8,128)} %copy-done.2) | copy-start | bytes 3145732
  231.5 4.3 %copy-start.11 = (f32[1,4096]{1,0:T(1,128)S(1)}, f32[1,4096]{1,0:T(1,128)}, u32[]{:S(2)}) copy-start(f32[1,4096]{1,0:T(1,128)} %param.18) | copy-start | bytes 49156
  235.7 9.4 %copy-start.1 = (bf16[256,2048]{1,0:T(8,128)(2,1)S(1)}, bf16[256,2048]{1,0:T(8,128)(2,1)}, u32[]{:S(2)}) copy-start(bf16[256,2048]{1,0:T(8,128)(2,1)} %param.10) | copy-start | bytes 3145732
where the time goes:
time: 246 us; the launch traced here: 245 us
  waiting for transfers between devices  119 us (48%)
  matrix products  36.1 us (15%)
  starting transfers between devices  30.3 us (12%)
  local copies, waits for them, and re-layouts  29.3 us (12%)
  other arithmetic  28.5 us (12%)
    ppermute x2, waiting for transfers between devices, layer_shard(): got_decay = lax.ppermute(acc_decay, 'sp', hop_pairs)  78.4 us
    ppermute x3, waiting for transfers between devices, layer_shard(): got_state = lax.ppermute(acc_state, 'sp', hop_pairs)  22.9 us
    ppermute x1, waiting for transfers between devices, layer_shard(): state_in = lax.ppermute(acc_state, 'sp', next_pairs)  18 us
    dot_general x1, matrix products, layer_shard(): jnp.dot(x, w_in, preferred_element_type=jnp.float32).astype(jnp.bfloat16)  17 us
    ppermute x3, starting transfers between devices, layer_shard(): got_state = lax.ppermute(acc_state, 'sp', hop_pairs)  13.4 us
    dot_general x1, matrix products, finish_layer(): jnp.dot(normed.reshape(n_tok, d_inner).astype(jnp.bfloat16), w_out, prefe...  9.39 us
    convert_element_type x1, other arithmetic, causal_conv(): return jax.nn.silu(pre_act).astype(jnp.bfloat16)  8.53 us
    add x3, other arithmetic, layer_shard(): acc_state = acc_decay[..., None, None] * got_state + acc_state  8.17 us
  transfers between devices with their start and end apart: 7, of which 4 were waited for; matrix products, arithmetic and copies ran while one was open for 11% of the time, Pallas kernels for 0%

commit v1 on v0

v1 whole, which is shorter than its diff:
```python
import functools
import jax
import jax.numpy as jnp
from jax import lax
from jax.experimental import pallas as pl
from jax.experimental.pallas import tpu as pltpu
from jax.sharding import PartitionSpec as P

NORM_EPS = 1e-5
LOG2E = 1.4426950408889634
F32 = jnp.float32
BF16 = jnp.bfloat16
LANES = 128
HALO = 16
TILE = 512
RING = 6
MESH = pl.DeviceIdType.MESH


def dot(lhs, rhs):
    return jnp.dot(lhs, rhs, preferred_element_type=F32)


def iota(shape, axis):
    return lax.broadcasted_iota(jnp.int32, shape, axis)


def split3(val):
    hi = val.astype(BF16)
    rest = val - hi.astype(F32)
    mid = rest.astype(BF16)
    low = (rest - mid.astype(F32)).astype(BF16)
    return hi, mid, low


def pack3(val):
    hi, mid, low = split3(val)
    first = hi.astype(F32) + pltpu.roll(mid.astype(F32), 64, axis=1)
    return jnp.concatenate([first.astype(BF16), low], axis=1)


def silu(val):
    half = 0.5 * val
    return half + half * jnp.tanh(half)


def layer_kernel(sizes, x_hbm, doc_ref, w_in_hbm, conv_w_ref, conv_b_ref, dt_bias_ref, a_log_ref, d_skip_ref, norm_w_ref, w_out_hbm,
                 out_ref,
                 w_buf, w_bcdt, w_out, x_own, x_t, doc_halo, p_x, p_bc, ho_x, ho_bc, hi_x, hi_bc, par, ub, xs, zs, ys, t_own, s_in, s_out, expand, bias, scores, taps,
                 w_end3, w_start3, a_grp, m_rows, rows_exp, b_t, c_64, sq_sum, normed,
                 w_sems, bc_sem, wo_sems, x_sem, halo_send, halo_recv, misc_send, misc_recv, state_send, state_recv):
    n_tok, d_model, d_inner, conv_dim, n_heads, state_dim, n_seq = sizes
    head_dim = d_inner // n_heads
    n_grp = d_inner // TILE
    per_grp = TILE // head_dim
    n_sub = TILE // LANES
    rank = lax.axis_index('sp')
    has_prev, has_next = rank > 0, rank < n_seq - 1
    lag = (rank // 2) * 3 + rank % 2
    max_lag = ((n_seq - 1) // 2) * 3 + (n_seq - 1) % 2
    conv_width = conv_w_ref.shape[0]

    n_early = 2

    def tile_col(step):
        x_col = d_inner + jnp.where(step == 0, 0, step - n_early) * TILE
        z_col = jnp.where(step <= n_early, step - 1, step - n_grp) * TILE
        is_x = (step == 0) | ((step > n_early) & (step < n_early + n_grp))
        return jnp.where(is_x, x_col, z_col)

    def tile_copy(step):
        slot = lax.rem(step, RING)
        return pltpu.make_async_copy(w_in_hbm.at[pl.ds(pl.multiple_of(tile_col(step), TILE), TILE)], w_buf.at[slot], w_sems.at[slot])

    def tile_start(step):
        @pl.when(step < 2 * n_grp)
        def _():
            tile_copy(step).start()

    def out_copy(step):
        rows = d_inner // n_grp
        return pltpu.make_async_copy(w_out_hbm.at[pl.ds(pl.multiple_of(step * rows, rows), rows)], w_out.at[pl.ds(pl.multiple_of(step * rows, rows), rows)], wo_sems.at[step])

    x_copy = pltpu.make_async_copy(x_hbm, x_own, x_sem)
    bc_copy = pltpu.make_async_copy(w_in_hbm.at[pl.ds(d_inner + d_inner, w_bcdt.shape[0])], w_bcdt, bc_sem)
    x_copy.start()
    bc_copy.start()
    for step in range(RING):
        tile_start(step)

    barrier = pltpu.get_barrier_semaphore()

    @pl.when(has_prev)
    def _():
        pl.semaphore_signal(barrier, inc=1, device_id={'sp': rank - 1}, device_id_type=MESH)

    @pl.when(has_next)
    def _():
        pl.semaphore_signal(barrier, inc=1, device_id={'sp': rank + 1}, device_id_type=MESH)
    pl.semaphore_wait(barrier, has_prev.astype(jnp.int32) + has_next.astype(jnp.int32))

    def to_next(src, dst, send_sem, recv_sem):
        return pltpu.make_async_remote_copy(src_ref=src, dst_ref=dst, send_sem=send_sem, recv_sem=recv_sem, device_id={'sp': rank + 1}, device_id_type=MESH)

    def x_halo(grp):
        return to_next(ho_x.at[grp], hi_x.at[grp], halo_send.at[grp], halo_recv.at[grp])

    def state_copy(grp):
        return to_next(s_out.at[grp], s_in.at[grp], state_send.at[grp], state_recv.at[grp])
    bc_halo = to_next(ho_bc, hi_bc, misc_send.at[0], misc_recv.at[0])
    d_halo = to_next(doc_ref.at[:, pl.ds(n_tok - LANES, LANES)], doc_halo, misc_send.at[1], misc_recv.at[1])

    @pl.when(has_next)
    def _():
        d_halo.start()

    @pl.when(jnp.logical_not(has_prev))
    def _():
        hi_x[...] = jnp.zeros_like(hi_x)
        hi_bc[...] = jnp.zeros_like(hi_bc)
        doc_halo[...] = jnp.zeros_like(doc_halo)
        s_in[...] = jnp.zeros_like(s_in)

    par[...] = jnp.zeros_like(par)
    par[0:1, 0:n_heads] = dt_bias_ref[...]
    par[1:2, 0:n_heads] = a_log_ref[...]
    par[2:3, 0:n_heads] = d_skip_ref[...]
    row_head = iota((4 * n_heads, TILE), 0)
    row_ok = row_head < 3 * n_heads
    row_head = lax.rem(row_head, n_heads)
    lane_head = iota((4 * n_heads, TILE), 1) // head_dim

    def expand_step(grp, carry):
        expand[grp] = jnp.where(row_ok & (row_head == lane_head + grp * per_grp), 1.0, 0.0).astype(BF16)
        return carry
    lax.fori_loop(0, n_grp, expand_step, 0)
    doc_row = doc_ref[...].astype(F32)
    tok_row, tok_lane = iota((n_tok, n_tok), 0), iota((n_tok, n_tok), 1)
    lower = tok_row >= tok_lane
    low_bf = jnp.where(lower, 1.0, 0.0).astype(BF16)
    up_bf = jnp.where(tok_row <= tok_lane, 1.0, 0.0).astype(BF16)
    seg_col = dot(jnp.where(lower, doc_row, 0.0).astype(BF16), jnp.ones((n_tok, n_tok), BF16))
    seg_row = dot(jnp.broadcast_to(doc_row, (8, n_tok)).astype(BF16), up_bf)[0:1]
    bias[...] = jnp.where(lower & (seg_col == seg_row), 0.0, -jnp.inf)

    def project(step):
        slot = lax.rem(step, RING)
        return dot(w_buf[slot], x_t[...]).astype(BF16).T

    def x_project(step, grp):
        tile_copy(step).wait()
        proj = project(step)
        p_x[lax.rem(grp, 2)] = proj
        ho_x[grp] = proj[n_tok - HALO:]
        tile_start(step + RING)

        @pl.when(has_next)
        def _():
            x_halo(grp).start()

    x_copy.wait()
    x_t[...] = x_own[...].T
    bc_copy.wait()
    p_bcdt = dot(w_bcdt[...], x_t[...]).astype(BF16)
    proj_bc = p_bcdt[0:2 * state_dim].T
    p_bc[...] = proj_bc
    ho_bc[...] = proj_bc[n_tok - HALO:]

    @pl.when(has_next)
    def _():
        bc_halo.start()
    x_project(0, 0)

    def early_step(step, carry):
        tile_copy(step).wait()
        zs[step - 1] = project(step)
        tile_start(step + RING)
        return carry
    lax.fori_loop(1, 1 + n_early, early_step, 0)

    @pl.when(has_prev)
    def _():
        bc_halo.wait_recv()
        d_halo.wait_recv()

    doc_ext = jnp.concatenate([doc_halo[...].astype(F32), doc_row], axis=1)
    ext_lane = iota((n_tok + 8, n_tok + LANES), 1)
    ext_ok = (ext_lane >= LANES - 8) & (ext_lane <= iota((n_tok + 8, n_tok + LANES), 0) + (LANES - 8))
    seg_ext = dot(jnp.where(ext_ok, doc_ext, 0.0).astype(BF16), jnp.ones((n_tok + LANES, LANES), BF16))
    for offset in range(1, conv_width):
        taps[offset - 1] = jnp.where(seg_ext[8:] == seg_ext[8 - offset:n_tok + 8 - offset], 1.0, 0.0)

    def conv_lane_tile(proj, halo, col, sub):
        ub[sub, pl.ds(0, 8), :] = halo[HALO - 8:].astype(F32)
        ub[sub, pl.ds(8, n_tok), :] = proj.astype(F32)
        lanes = pl.ds(col, LANES)
        acc = conv_b_ref[:, lanes] + conv_w_ref[0:1, lanes] * ub[sub, pl.ds(8, n_tok), :]
        for offset in range(1, conv_width):
            acc = acc + conv_w_ref[offset:offset + 1, lanes] * (taps[offset - 1] * ub[sub, pl.ds(8 - offset, n_tok), :])
        return silu(acc).astype(BF16)

    bc = conv_lane_tile(p_bc[...], hi_bc[...], d_inner, 0).astype(F32)
    b_t[...] = bc.T[0:state_dim].astype(BF16)
    c_64[...] = pltpu.roll(bc, 64, axis=1)[:, 0:state_dim].astype(BF16)
    scores[...] = dot(c_64[...], b_t[...])
    par_t = par[...].T
    pre_dt = p_bcdt[2 * state_dim:].astype(F32) + par_t[0:n_heads, 0:1]
    dt_val = jnp.maximum(pre_dt, 0.0) + jnp.log1p(jnp.exp(-jnp.abs(pre_dt)))
    log_decay = -jnp.exp(par_t[0:n_heads, 1:2]) * dt_val
    hi, mid, low = split3(log_decay)
    cum = (dot(low, up_bf) + dot(mid, up_bf)) + dot(hi, up_bf)
    cum2 = cum * LOG2E
    m_rows[...] = jnp.log2(dt_val) - cum2
    last_cum, seg_last = cum[:, n_tok - 1:n_tok], seg_row[:, n_tok - 1:n_tok]
    w_end = jnp.where(seg_row == seg_last, jnp.exp(last_cum - cum) * dt_val, 0.0)
    w_start = jnp.where(seg_row == 0.0, jnp.exp(cum), 0.0)
    pad = jnp.zeros((LANES - n_heads, n_tok), F32)
    cum2_col = jnp.concatenate([cum2, pad], axis=0).T
    for grp in range(n_grp):
        a_grp[grp] = pltpu.roll(cum2_col, (LANES - grp * per_grp) % LANES, axis=1)
    w_end3[...] = pack3(jnp.concatenate([w_end, pad], axis=0).T)
    start_col = jnp.concatenate([w_start, pad], axis=0).T
    w_start3[...] = pack3(start_col)
    rows2 = pack3(jnp.concatenate([start_col[n_tok - 1:n_tok], par[2:3, :], jnp.zeros((6, LANES), F32)], axis=0))

    def rows_step(grp, carry):
        rows_exp[grp] = dot(rows2, expand[grp])
        return carry
    lax.fori_loop(0, n_grp, rows_step, 0)

    def serve(slot):
        grp = slot - lag

        @pl.when((grp >= 0) & (grp < n_grp))
        def _():
            @pl.when(has_prev)
            def _():
                state_copy(grp).wait_recv()

            @pl.when(has_next)
            def _():
                s_out[grp] = rows_exp[grp, 0:1, :] * s_in[grp] + t_own[grp]
                state_copy(grp).start()

    def x_step(grp, carry):
        @pl.when(grp < n_grp - 1)
        def _():
            x_project(grp + 1 + n_early, grp + 1)

        @pl.when(has_prev)
        def _():
            x_halo(grp).wait_recv()
        proj, halo = p_x[lax.rem(grp, 2)], hi_x[grp]
        weight = dot(w_end3[...], expand[grp])
        scaled = []
        for sub in range(n_sub):
            xv = conv_lane_tile(proj[:, sub * LANES:(sub + 1) * LANES], halo[:, sub * LANES:(sub + 1) * LANES], pl.multiple_of(grp * TILE + sub * LANES, LANES), sub)
            xs[grp, :, pl.ds(sub * LANES, LANES)] = xv
            scaled.append((xv.astype(F32) * weight[:, sub * LANES:(sub + 1) * LANES]).astype(BF16))
        t_own[grp] = dot(b_t[...], jnp.concatenate(scaled, axis=1))
        serve(grp)
        return carry
    lax.fori_loop(0, n_grp, x_step, 0)

    pair_lane = iota((n_tok, LANES), 1) < head_dim

    def intra(grp):
        a_cols = a_grp[grp]
        m_grp = m_rows[pl.ds(pl.multiple_of(grp * per_grp, per_grp), per_grp), :]
        cb, bs = scores[...], bias[...]
        skip = rows_exp[grp, 1:2, :]
        for pair in range(per_grp // 2):
            lanes = pl.ds(pair * LANES, LANES)
            x_pair = xs[grp, :, lanes]
            mixes = []
            for head in (2 * pair, 2 * pair + 1):
                expo = (a_cols[:, head:head + 1] + m_grp[head:head + 1, :]) + bs
                mixes.append((cb * jnp.exp2(expo)).astype(BF16))
            zero = jnp.zeros_like(x_pair)
            both = jnp.concatenate([jnp.where(pair_lane, x_pair, zero), jnp.where(pair_lane, zero, x_pair)], axis=0)
            ys[grp, :, lanes] = dot(jnp.concatenate(mixes, axis=1), both) + skip[:, pair * LANES:(pair + 1) * LANES] * x_pair.astype(F32)

    def zy_step(grp, carry):
        step = grp + n_grp + n_early
        tile_copy(step).wait()
        zs[grp + n_early] = project(step)
        out_copy(grp).start()
        intra(grp)
        serve(grp + n_grp)
        return carry
    lax.fori_loop(0, n_grp - n_early, zy_step, 0)

    def y_step(grp, carry):
        out_copy(grp).start()
        intra(grp)
        serve(grp + n_grp)
        return carry
    lax.fori_loop(n_grp - n_early, n_grp, y_step, 0)
    for slot in range(2 * n_grp, n_grp + max_lag):
        serve(slot)

    sq_sum[...] = jnp.zeros_like(sq_sum)

    def gate_step(grp, carry):
        from_state = dot(c_64[...], s_in[grp].astype(BF16))
        weight = dot(w_start3[...], expand[grp])
        gated = (ys[grp] + from_state * weight) * silu(zs[grp].astype(F32))
        ys[grp] = gated
        sq = gated * gated
        acc = sq_sum[...]
        for sub in range(n_sub):
            acc = acc + sq[:, sub * LANES:(sub + 1) * LANES]
        sq_sum[...] = acc
        return carry
    lax.fori_loop(0, n_grp, gate_step, 0)

    scale = lax.rsqrt(jnp.sum(sq_sum[...], axis=1, keepdims=True) / d_inner + NORM_EPS)

    def norm_step(grp, carry):
        cols = pl.ds(pl.multiple_of(grp * TILE, TILE), TILE)
        normed[:, cols] = (ys[grp] * scale * norm_w_ref[:, cols]).astype(BF16)
        out_copy(grp).wait()
        return carry
    lax.fori_loop(0, n_grp, norm_step, 0)

    def out_step(col, carry):
        cols = pl.ds(pl.multiple_of(col * TILE, TILE), TILE)
        out_ref[:, cols] = dot(normed[...], w_out[:, cols]).astype(BF16)
        return carry
    lax.fori_loop(0, d_model // TILE, out_step, 0)

    @pl.when(has_next)
    def _():
        d_halo.wait_send()
        bc_halo.wait_send()
        for grp in range(n_grp):
            x_halo(grp).wait_send()
            state_copy(grp).wait_send()


def solution(mesh):
    n_seq = mesh.shape['sp']
    row_spec = P(('dp', 'sp'), None)
    tok_spec = P(('dp', 'sp'))

    def layer_shard(x, doc_start, w_in, conv_w, conv_b, dt_bias, a_log, d_skip, norm_w, w_out):
        n_tok, d_model = x.shape
        d_inner = w_out.shape[0]
        conv_dim = conv_w.shape[1]
        n_heads = a_log.shape[0]
        state_dim = (conv_dim - d_inner) // 2
        n_grp = d_inner // TILE
        sizes = (n_tok, d_model, d_inner, conv_dim, n_heads, state_dim, n_seq)
        vmem = pl.BlockSpec(memory_space=pltpu.VMEM)
        hbm = pl.BlockSpec(memory_space=pl.ANY)
        return pl.pallas_call(
            functools.partial(layer_kernel, sizes),
            out_shape=jax.ShapeDtypeStruct((n_tok, d_model), BF16),
            in_specs=[hbm, vmem, hbm, vmem, vmem, vmem, vmem, vmem, vmem, hbm],
            out_specs=vmem,
            scratch_shapes=[
                pltpu.VMEM((RING, TILE, d_model), BF16),
                pltpu.VMEM((2 * state_dim + n_heads, d_model), BF16),
                pltpu.VMEM((d_inner, d_model), BF16),
                pltpu.VMEM((n_tok, d_model), BF16),
                pltpu.VMEM((d_model, n_tok), BF16),
                pltpu.VMEM((1, LANES), jnp.int32),
                pltpu.VMEM((2, n_tok, TILE), BF16),
                pltpu.VMEM((n_tok, 2 * state_dim), BF16),
                pltpu.VMEM((n_grp, HALO, TILE), BF16),
                pltpu.VMEM((HALO, 2 * state_dim), BF16),
                pltpu.VMEM((n_grp, HALO, TILE), BF16),
                pltpu.VMEM((HALO, 2 * state_dim), BF16),
                pltpu.VMEM((LANES, LANES), F32),
                pltpu.VMEM((TILE // LANES, n_tok + 8, LANES), F32),
                pltpu.VMEM((n_grp, n_tok, TILE), BF16),
                pltpu.VMEM((n_grp, n_tok, TILE), BF16),
                pltpu.VMEM((n_grp, n_tok, TILE), F32),
                pltpu.VMEM((n_grp, state_dim, TILE), F32),
                pltpu.VMEM((n_grp, state_dim, TILE), F32),
                pltpu.VMEM((n_grp, state_dim, TILE), F32),
                pltpu.VMEM((n_grp, 4 * n_heads, TILE), BF16),
                pltpu.VMEM((n_tok, n_tok), F32),
                pltpu.VMEM((n_tok, n_tok), F32),
                pltpu.VMEM((conv_w.shape[0] - 1, n_tok, LANES), F32),
                pltpu.VMEM((n_tok, 2 * LANES), BF16),
                pltpu.VMEM((n_tok, 2 * LANES), BF16),
                pltpu.VMEM((n_grp, n_tok, LANES), F32),
                pltpu.VMEM((n_heads, n_tok), F32),
                pltpu.VMEM((n_grp, 8, TILE), F32),
                pltpu.VMEM((state_dim, n_tok), BF16),
                pltpu.VMEM((n_tok, state_dim), BF16),
                pltpu.VMEM((n_tok, LANES), F32),
                pltpu.VMEM((n_tok, d_inner), BF16),
                pltpu.SemaphoreType.DMA((RING,)),
                pltpu.SemaphoreType.DMA,
                pltpu.SemaphoreType.DMA((n_grp,)),
                pltpu.SemaphoreType.DMA,
                pltpu.SemaphoreType.DMA((n_grp,)),
                pltpu.SemaphoreType.DMA((n_grp,)),
                pltpu.SemaphoreType.DMA((2,)),
                pltpu.SemaphoreType.DMA((2,)),
                pltpu.SemaphoreType.DMA((n_grp,)),
                pltpu.SemaphoreType.DMA((n_grp,)),
            ],
            compiler_params=pltpu.CompilerParams(collective_id=0, has_side_effects=True, vmem_limit_bytes=67043328),
        )(x, doc_start[None, :], w_in.T, conv_w, conv_b[None, :], dt_bias[None, :], a_log[None, :], d_skip[None, :], norm_w, w_out)

    return jax.shard_map(layer_shard, mesh=mesh, in_specs=(row_spec, tok_spec, P(), P(), P(), P(), P(), P(), P(), P()), out_specs=row_spec, check_vma=False)
```

time: 246 us -> 52.1 us (0.21)
  the two profiles are of different devices: /device:TPU:113 before, /device:TPU:127 now
where the time goes in v1:
time: 52.1 us; the launch traced here: 51.9 us
  Pallas kernels  48.2 us (93%)
  local copies, waits for them, and re-layouts  3.65 us (7%)
    pallas_call x1, Pallas kernels, layer_shard(): pl.pallas_call(functools.partial(layer_kernel, sizes), out_shape=jax.Shap...  48.2 us
    unnamed x1, local copies, waits for them, and re-layouts  2.3 us
    broadcast_in_dim x1, local copies, waits for them, and re-layouts, layer_shard(): conv_b[None, :]  1.34 us

profile of v1, /device:TPU:127, one launch (start us, length us, event | category | flops | bytes accessed | tf_op | source)
XLA Modules:
  0.0 51.9 jit_solution(3743697479122869410)
XLA Ops:
  0.0 1.3 %broadcast_in_dim.16.conv_b_ref = f32[1,4224]{1,0:T(1,128)} reshape(f32[4224]{0:T(1024)} %param.14) | data formatting | bytes 33792 | tf_op jit(solution)/shard_map/broadcast_in_dim | solution.py:407
  1.3 48.2 %shard_map.100 = bf16[256,2048]{1,0:T(8,128)(2,1)} custom-call(bf16[256,2048]{1,0:T(8,128)(2,1)} %x_hbm.1, s32[1,256]{1,0:T(1,128)} %bitcast.6, bf16[8384,2048]{1,0:T(8,128)(2,1)} %bitcast.5, f32[4,4224]{1,0:T(4,128)} %conv_w_ref.1, f32[1,4224]{1,0:T(1,128)} %broadcast_in_dim.16.conv_b_ref, f32[1,64]{1,0:T(1,128)} %bitcast.7, f32[1,64]{1,0:T(1,128)} %bitcast.8, ...), custom_call_target="tpu_custom_call" | custom-call | tf_op jit(solution)/shard_map/pallas_call | solution.py:356
  49.6 2.3 %copy.12 = bf16[256,2048]{1,0:T(8,128)(2,1)} copy(bf16[256,2048]{1,0:T(8,128)(2,1)} %shard_map.100) | data formatting | bytes 2097152
